TPU v7x, 512 devices: a 4x2x32 block of a 4x16x32 slice. The times are simulated.
512 devices in a mesh: group: 2 (over y), expert: 32 (over z), tensor: 4 (over x), sub: 2 (over core).
Axes of the slice: x: 4, y: 2, z: 32, core: 2. Of those that a mesh axis runs over, the one named last changes fastest.
The devices are a block of a 4x16x32 slice.
Arguments:
- tokens: bfloat16 [512, 7168], P(('group', 'expert', 'sub')), parts along dimension 0, may hold values from -6 to 6
- expert_ids: int32 [512, 8], P(('group', 'expert', 'sub')), parts along dimension 0, may hold values from 0 to 15, all different within a row; in each aligned block of 4 rows (0 to 3, 4 to 7, ...) at most 3 rows name the same one
- gate_codes: int32 [512, 8], P(('group', 'expert', 'sub')), parts along dimension 0, may hold values from 1 to 63
- w_gate: bfloat16 [32, 1024, 7168], P('expert', ('tensor', 'sub')), may hold values from -0.0625 to 0.0625
- w_up: bfloat16 [32, 1024, 7168], P('expert', ('tensor', 'sub')), may hold values from -0.0625 to 0.0625
- w_down: bfloat16 [32, 1024, 7168], P('expert', ('tensor', 'sub')), may hold values from -0.125 to 0.125
Outputs:
- mixed: bfloat16 [512, 7168], P(('group', 'expert', 'sub'), 'tensor'), parts along dimension 0
There are 2 independent parts, one for each index of `group`. A program takes and returns all parts, laid end to end along the dimension named above; an argument that names none is the same for every part. Nothing has to cross between parts.
Inputs may be any that keep to these rules, and one draw needn't show every extreme that they name: `expert_ids`: the 8 numbers of a row differ; within the rows of one device (aligned blocks of 4 rows) no expert is named by more than 3 rows, a bound that some block reaches.
All inputs are finite; a program needn't handle non-finite values.
Results may differ from a plain program's by a relative error of at most 0.008.
Values may be sent and summed in bfloat16 or wider, within the bound.
A program may use at most 64 MiB of HBM per device.

v0:
```python
import jax
import jax.numpy as jnp
from jax import lax
from jax.sharding import PartitionSpec as P


def shards(tokens, expert_ids, gate_codes, w_gate, w_up, w_down):
    tok_rows, features = tokens.shape
    per_token = expert_ids.shape[1]
    owners = lax.axis_size("expert")
    sub_count = lax.axis_size("sub")
    tensor_count = lax.axis_size("tensor")
    experts = owners // 2
    capacity = min(tok_rows, tok_rows * per_token // experts + 1)
    flat_ids = expert_ids.reshape(-1)
    matches = (flat_ids[:, None] == jnp.arange(experts, dtype=jnp.int32)[None, :]).astype(jnp.int32)
    before = jnp.cumsum(matches, axis=0) - matches
    slot_index = jnp.sum(before * matches, axis=1)
    position = flat_ids * capacity + slot_index
    onehot = position[:, None] == jnp.arange(experts * capacity, dtype=jnp.int32)[None, :]
    weights = gate_codes.reshape(-1).astype(jnp.float32) / 64.0
    choose = jnp.any(onehot.reshape(tok_rows, per_token, -1), axis=1).astype(jnp.bfloat16)
    combine = jnp.sum(
        jnp.where(onehot, weights[:, None], 0.0).reshape(tok_rows, per_token, -1), axis=1
    )
    packed = jnp.dot(choose.T, tokens, preferred_element_type=jnp.float32).astype(jnp.bfloat16)
    outgoing = jnp.broadcast_to(
        packed.reshape(experts, 1, capacity, features), (experts, 2, capacity, features)
    )
    arrived = lax.all_to_all(
        outgoing.reshape(owners, capacity, features),
        "expert",
        split_axis=0,
        concat_axis=0,
        tiled=True,
    )
    slot_rows = lax.all_gather(arrived, "sub", axis=1, tiled=True).reshape(-1, features)
    contract = (((1,), (1,)), ((), ()))
    gate_act = lax.dot_general(slot_rows, w_gate[0], contract, preferred_element_type=jnp.float32)
    up_act = lax.dot_general(slot_rows, w_up[0], contract, preferred_element_type=jnp.float32)
    hidden = (jax.nn.silu(gate_act) * up_act).astype(jnp.bfloat16)
    partial_value = jnp.dot(hidden, w_down[0], preferred_element_type=jnp.float32).astype(
        jnp.bfloat16
    )
    partial_value = partial_value.reshape(owners, sub_count, capacity, features)
    block = features // tensor_count
    sectioned = partial_value.reshape(owners, sub_count, capacity, tensor_count, block).transpose(
        0, 2, 3, 1, 4
    )
    sectioned = sectioned.reshape(owners, capacity, tensor_count * sub_count, block)
    gathered = lax.all_to_all(sectioned, ("tensor", "sub"), split_axis=2, concat_axis=2, tiled=True)
    run_total = jnp.sum(gathered.astype(jnp.float32), axis=2)
    came_back = lax.all_to_all(
        run_total.astype(jnp.bfloat16), "expert", split_axis=0, concat_axis=0, tiled=True
    ).astype(run_total.dtype)
    summed = jnp.sum(came_back.reshape(experts, 2, capacity, block), axis=1)
    mixed = jnp.dot(
        combine,
        summed.reshape(-1, block),
        precision=lax.Precision.HIGHEST,
        preferred_element_type=jnp.float32,
    )
    return mixed.astype(jnp.bfloat16)


def solution(mesh):
    return jax.shard_map(
        shards,
        mesh=mesh,
        in_specs=(
            P(("group", "expert", "sub"), None),
            P(("group", "expert", "sub"), None),
            P(("group", "expert", "sub"), None),
            P("expert", ("tensor", "sub"), None),
            P("expert", ("tensor", "sub"), None),
            P("expert", ("tensor", "sub"), None),
        ),
        out_specs=P(("group", "expert", "sub"), "tensor"),
        check_vma=False,
    )
```

profile of v0, /device:TPU:33, one launch (start us, length us, event | category | flops | bytes accessed | tf_op | source)
XLA Modules:
  0.0 407.3 jit_solution(4467936220724837105)
XLA Ops:
  6.5 0.0 copy-start
  6.6 0.0 all-gather.2.cloned.1.call-start
  6.6 0.9 eq.30
  7.4 0.1 fusion.20
  7.5 0.1 reduce_window_sum.11
  7.6 0.2 select_reduce_fusion.1
  7.8 0.1 reduce_sum.42
  7.8 0.7 multiply_add_fusion
  8.5 0.1 fusion.19
  8.6 1.2 convolution_convert_fusion.1
  9.8 0.4 broadcast_in_dim.25
  10.3 0.5 broadcast_in_dim.26
  10.8 221.9 %all_to_all.15 = bf16[32,3,7168]{2,1,0:T(4,128)(2,1)S(1)} all-to-all(bf16[32,3,7168]{2,1,0:T(4,128)(2,1)S(1)} %bitcast.29), channel_id=1, replica_groups=mesh['group'=2,'expert'=32,'tensor'=4,'sub'=2] {'expert'}, dimensions={0} | all-to-all | bytes 2752512 | tf_op jit(solution)/shard_map/all_to_all | solution.py:30
  232.7 1.6 copy.21
  234.3 0.1 all-gather.2.cloned.1.call-update
  234.4 16.4 %all-gather.2.cloned.1.call-done = bf16[32,6,7168]{2,0,1:T(8,128)(2,1)} async-done(((bf16[32,3,7168]{2,0,1:T(8,128)(2,1)}), bf16[32,6,7168]{2,0,1:T(8,128)(2,1)}) %all-gather.2.cloned.1.call-update) | async-done | bytes 2752528 | tf_op jit(solution)/shard_map/all_gather | solution.py:37
  250.8 5.1 %copy.22 = bf16[32,6,7168]{2,1,0:T(8,128)(2,1)} copy(bf16[32,6,7168]{2,0,1:T(8,128)(2,1)} %all-gather.2.cloned.1.call-done) | data formatting | bytes 5505024 | tf_op jit(solution)/shard_map/all_gather | solution.py:37
  255.9 4.6 %reshape.60 = bf16[192,7168]{1,0:T(8,128)(2,1)} reshape(bf16[32,6,7168]{2,1,0:T(8,128)(2,1)} %copy.22) | data formatting | bytes 5505024 | tf_op jit(solution)/shard_map/reshape | solution.py:37
  260.6 3.2 fusion.3
  263.8 0.0 copy-done
  263.8 7.0 %convolution_convert_fusion = bf16[192,7168]{1,0:T(8,128)(2,1)} fusion(bf16[1,128,7168]{2,1,0:T(8,128)(2,1)S(1)} %copy-done, bf16[192,7168]{1,0:T(8,128)(2,1)} %reshape.60, bf16[1,128,7168]{2,1,0:T(8,128)(2,1)} %param.10, f32[192,128]{1,0:T(8,128)S(1)} %fusion.3), kind=kOutput, calls=%fused_computation | convolution fusion | flops 706166784 | bytes 9273344 | tf_op jit(solution)/shard_map/dot_general | solution.py:42
  270.7 6.2 %reshape_reshape.3 = bf16[32,2,3,4,1792]{4,3,2,1,0:T(4,128)(2,1)} reshape(bf16[192,7168]{1,0:T(8,128)(2,1)} %convolution_convert_fusion) | data formatting | bytes 5505024 | tf_op jit(solution)/shard_map/reshape;reshape | solution.py:47
  276.9 2.3 copy.29
  279.3 36.9 %all_to_all.16 = bf16[32,3,8,1792]{3,0,1,2:T(8,128)(2,1)} all-to-all(bf16[32,3,8,1792]{3,0,1,2:T(8,128)(2,1)S(1)} %bitcast.28), channel_id=1, replica_groups=mesh['group'=2,'expert'=32,'tensor'=4,'sub'=2] {'tensor','sub'}, dimensions={2} | all-to-all | bytes 5505024 | tf_op jit(solution)/shard_map/all_to_all | solution.py:51
  316.1 0.0 copy-start.1
  316.1 2.2 reduce_sum.44
  318.4 1.1 copy.26
  319.4 22.1 %all-to-all-start.2 = ((bf16[32,3,1792]{2,1,0:T(4,128)(2,1)}), bf16[32,3,1792]{2,1,0:T(4,128)(2,1)S(1)}, u32[]{:S(2)}, u32[]{:S(2)}) async-start(bf16[32,3,1792]{2,1,0:T(4,128)(2,1)} %copy.26), calls=%async_computation.2 | async-start | bytes 917504 | tf_op jit(solution)/shard_map/all_to_all | solution.py:53
  341.5 0.0 copy-done.1
  341.6 0.1 select_reduce_fusion
  341.7 57.5 %all-to-all-done.2 = bf16[32,3,1792]{2,1,0:T(4,128)(2,1)S(1)} async-done(((bf16[32,3,1792]{2,1,0:T(4,128)(2,1)}), bf16[32,3,1792]{2,1,0:T(4,128)(2,1)S(1)}, u32[]{:S(2)}, u32[]{:S(2)}) %all-to-all-start.2) | async-done | bytes 344096 | tf_op jit(solution)/shard_map/all_to_all | solution.py:53
  399.1 0.3 convert_reduce_fusion
  399.4 0.2 reshape.64
  399.6 0.9 convolution_convert_fusion.2
  (1 shorter events, 0.0 us)
Async XLA Ops:
  6.5 257.2 %copy-start = (bf16[1,128,7168]{2,1,0:T(8,128)(2,1)S(1)}, bf16[1,128,7168]{2,1,0:T(8,128)(2,1)}, u32[]{:S(2)}) copy-start(bf16[1,128,7168]{2,1,0:T(8,128)(2,1)} %param.11) | copy-start | bytes 5505028
  6.6 244.3 %all-gather.2.cloned.1.call-start = ((), (), s32[]{:S(2)}) async-start(), calls=%async_computation.3 | async-start | bytes 4128768 | tf_op jit(solution)/shard_map/all_gather | solution.py:37
  316.1 25.4 %copy-start.1 = (s32[4,8]{1,0:T(4,128)S(1)}, s32[4,8]{1,0:T(4,128)}, u32[]{:S(2)}) copy-start(s32[4,8]{1,0:T(4,128)} %param.8) | copy-start | bytes 388
  319.4 79.7 %all-to-all-start.2 = ((bf16[32,3,1792]{2,1,0:T(4,128)(2,1)}), bf16[32,3,1792]{2,1,0:T(4,128)(2,1)S(1)}, u32[]{:S(2)}, u32[]{:S(2)}) async-start(bf16[32,3,1792]{2,1,0:T(4,128)(2,1)} %copy.26), calls=%async_computation.2 | async-start | bytes 917504 | tf_op jit(solution)/shard_map/all_to_all | solution.py:53
Sparse Core Ops, SparseCore 0:
  234.5 16.2 all-gather.1
where the time goes:
time: 408 us; the launch traced here: 407 us
  blocking collectives  259 us (63%)
  waiting for transfers between devices  74 us (18%)
  local copies, waits for them, and re-layouts  23.1 us (6%)
  starting transfers between devices  22.1 us (5%)
  between operations  13.5 us (3%)
  matrix products  12.2 us (3%)
    all_to_all x1, blocking collectives, shards(): lax.all_to_all(outgoing.reshape(owners, capacity, features), 'expert', sp...  222 us
    all_to_all x1, waiting for transfers between devices, shards(): lax.all_to_all(run_total.astype(jnp.bfloat16), 'expert', split_axis=0, co...  57.5 us
    all_to_all x1, blocking collectives, shards(): lax.all_to_all(sectioned, ('tensor', 'sub'), split_axis=2, concat_axis=2,...  36.9 us
    all_to_all x1, starting transfers between devices, shards(): lax.all_to_all(run_total.astype(jnp.bfloat16), 'expert', split_axis=0, co...  22.1 us
    all_gather x1, waiting for transfers between devices, shards(): lax.all_gather(arrived, 'sub', axis=1, tiled=True).reshape(-1, features)  16.4 us
  transfers between devices with their start and end apart: 2, of which 2 were waited for; matrix products, arithmetic and copies ran while one was open for 0% of the time, Pallas kernels for 0%

commit v1 on v0

v1 whole, which is shorter than its diff:
```python
import functools

import jax
import jax.numpy as jnp
from jax import lax
from jax.experimental import pallas as pl
from jax.experimental.pallas import tpu as pltpu
from jax.sharding import PartitionSpec as P

MESH = pl.DeviceIdType.MESH
STRIDE = 4
LANES = 128
F32 = jnp.float32
BF16 = jnp.bfloat16


def plan(owners):
    last = owners // (2 * STRIDE)
    waves, rings = [], []
    for s in range(last + 1):
        d = STRIDE * s
        if s == 0:
            ring, near = [0], [1, -1, 2, -2]
        elif s < last:
            ring, near = [-d, d], [1 - d, 1 + d, -1 - d, -1 + d, -2 - d, 2 + d]
        else:
            ring, near = [d], [1 + d, -1 + d]
        rings.append(len(ring))
        waves.append([v % owners for v in ring + near])
    base = [0] + [v for s in range(1, last) for v in (-STRIDE * s, STRIDE * s)] + [STRIDE * last]
    order = base + [v + 1 for v in base] + [v - 1 for v in base]
    order += [2 + STRIDE * s for s in range(last)] + [-2 - STRIDE * s for s in range(last)]
    return waves, rings, base, [v % owners for v in order]


def kernel(
    owners, tensors, placed, w_gate, w_up, w_down, out,
    z_buf, partner_in, x_buf, c_buf, gu, dn, act, own, p_send, p_recv, s_buf, via, r_buf,
    near, far_send, far, fin, fin_recv,
    load, send, swap, ring_p, ring_m, local, x_in, x_fwd, c_in, pc, via_in, r_in, near_in, far_in, fin_in,
):
    waves, rings, base, order = plan(owners)
    last = len(waves) - 1
    flat = [v for wave in waves for v in wave]
    slot = {v: i for i, v in enumerate(flat)}
    starts = [sum(len(w) for w in waves[:s]) for s in range(last + 2)]
    place = {v: i for i, v in enumerate(order)}
    width = x_buf.shape[-1]
    rows = owners * z_buf.shape[1]
    runs = w_gate.shape[1]
    z, x, c = lax.axis_index("expert"), lax.axis_index("tensor"), lax.axis_index("sub")

    def at_z(d):
        return {"expert": lax.rem(z + (d % owners), owners)}

    def at_x(d):
        return {"tensor": lax.rem(x + (d % tensors), tensors)}

    partner = {"sub": 1 - c}

    def block_of(d, other):
        return lax.rem(x + (d % tensors), tensors) * 2 + (1 - c if other else c)

    loads = []
    for b in range(gu.shape[0]):
        cols = pl.ds(b * width, width)
        for src, dst in (
            (w_gate.at[0, :, cols], gu.at[b, 0:runs]),
            (w_up.at[0, :, cols], gu.at[b, runs : 2 * runs]),
            (w_down.at[0, :, cols], dn.at[b]),
        ):
            loads.append(pltpu.make_async_copy(src, dst, load.at[len(loads)]))
    for cp in loads:
        cp.start()

    peers = [at_z(d) for d in (STRIDE, -STRIDE, 1, -1, 2, -2)] + [at_x(1), at_x(-1), partner]
    barrier = pltpu.get_barrier_semaphore()
    for peer in peers:
        pl.semaphore_signal(barrier, inc=1, device_id=peer, device_id_type=MESH)
    pl.semaphore_wait(barrier, len(peers))

    sent = []

    def push(src, dst, sem, target):
        cp = pltpu.make_async_remote_copy(
            src_ref=src, dst_ref=dst, send_sem=send.at[len(sent)], recv_sem=sem,
            device_id=target, device_id_type=MESH,
        )
        cp.start()
        sent.append(cp)

    def arrive(ref, sem):
        pltpu.make_async_remote_copy(
            src_ref=ref, dst_ref=ref, send_sem=sem, recv_sem=sem,
            device_id=partner, device_id_type=MESH,
        ).wait_recv()

    push(placed.at[block_of(0, True)], partner_in, swap, partner)
    arrive(partner_in, swap)
    z_buf[0] = (placed[block_of(0, False)].astype(F32) + partner_in[...].astype(F32)).astype(BF16)

    def z_at(v):
        return z_buf.at[slot[v % owners]]

    def span(buf, s, lo=0, hi=None):
        hi = len(waves[s]) if hi is None else hi
        return buf.at[pl.ds(starts[s] + lo, hi - lo)]

    def z_part(s):
        return z_buf.at[pl.ds(starts[s], len(waves[s])), :, pl.ds(0, width)]

    def spread(v, up, down):
        push(z_at(v), z_at(v - 1), local.at[up], at_z(1))
        push(z_at(v), z_at(v + 1), local.at[up], at_z(-1))
        if down <= 0 and up < last:
            push(z_at(v), z_at(v - 2), local.at[up], at_z(2))
        if down >= 0 and up < last:
            push(z_at(v), z_at(v + 2), local.at[up], at_z(-2))

    def cut(s):
        n = len(waves[s])
        return n // 2 if s < last else n - n // 2

    def forward_x(s):
        arrive(span(x_buf.at[0], s), x_in.at[0, s])
        push(span(x_buf.at[0], s, 0, cut(s)), span(x_buf.at[2], s, 0, cut(s)), x_fwd.at[0, s], at_x(1))
        arrive(span(x_buf.at[1], s), x_in.at[1, s])
        push(span(x_buf.at[1], s, cut(s)), span(x_buf.at[2], s, cut(s)), x_fwd.at[1, s], at_x(-1))
        for i in (0, 1):
            push(span(x_buf.at[i], s), span(c_buf.at[1 + i], s), c_in.at[1 + i, s], partner)

    def finish_x(s):
        arrive(span(x_buf.at[2], s, 0, cut(s)), x_fwd.at[0, s])
        arrive(span(x_buf.at[2], s, cut(s)), x_fwd.at[1, s])
        push(span(x_buf.at[2], s), span(c_buf.at[3], s), c_in.at[3, s], partner)

    for s in range(last + 1):
        d = STRIDE * s
        if s > 0:
            arrive(z_at(-d), ring_p.at[s])
        if s < last:
            push(z_at(-d), z_at(-d - STRIDE), ring_p.at[s + 1], at_z(STRIDE))
        if 0 < s < last:
            arrive(z_at(d), ring_m.at[s])
        if s < last - 1:
            push(z_at(d), z_at(d + STRIDE), ring_m.at[s + 1], at_z(-STRIDE))
        if s == 0 or s == last:
            spread(d, s, 0)
        else:
            spread(-d, s, -1)
            spread(d, s, 1)
        arrive(span(z_buf, s, rings[s]), local.at[s])
        push(z_part(s), span(x_buf.at[0], s), x_in.at[0, s], at_x(1))
        push(z_part(s), span(x_buf.at[1], s), x_in.at[1, s], at_x(-1))
        push(z_part(s), span(c_buf.at[0], s), c_in.at[0, s], partner)
        if s >= 1:
            forward_x(s - 1)
        if s >= 2:
            finish_x(s - 2)

    for cp in loads:
        cp.wait()

    def multiply(ref, b, first=False):
        value = ref.astype(F32).reshape(rows, width).astype(BF16)
        part = lax.dot_general(value, gu[b], (((1,), (1,)), ((), ())), preferred_element_type=F32)
        act[...] = part if first else act[...] + part

    multiply(z_buf[:, :, 0:width], block_of(0, False), True)
    forward_x(last)
    finish_x(last - 1)
    multiply(x_buf[0], block_of(-1, False))
    multiply(x_buf[1], block_of(1, False))
    finish_x(last)
    for i, d in enumerate((0, -1, 1, 2)):
        for s in range(last + 1):
            arrive(span(c_buf.at[i], s), c_in.at[i, s])
        multiply(c_buf[i], block_of(d, True))
    multiply(x_buf[2], block_of(2, False))

    shares = z_buf[:, :, width:].astype(F32).reshape(rows, LANES)
    lane = lax.broadcasted_iota(jnp.int32, (rows, LANES), 1)
    share = jnp.sum(jnp.where(lane == z // 2, shares, 0.0), axis=1, keepdims=True)
    gate, up = act[:, 0:runs], act[:, runs:]
    hidden = (gate / (1.0 + jnp.exp(-gate)) * up * share).astype(BF16)

    def down(b):
        part = jnp.dot(hidden, dn[b], preferred_element_type=F32)
        return part.reshape(owners, rows // owners, width)

    steps = (2, 1, -1, 0)
    for i, d in enumerate(steps):
        part = down(block_of(d, True)).astype(BF16)
        for j, v in enumerate(flat):
            p_send[i, place[v]] = part[j]
        push(p_send.at[i], p_recv.at[i], pc.at[i], partner)
    for i, d in enumerate(steps):
        part = down(block_of(d, False))
        for j, v in enumerate(flat):
            own[i, place[v]] = part[j]

    half = owners // 2
    lo, hi = pl.ds(0, half), pl.ds(half, half)

    def both(i, part):
        return own[i, part] + p_recv[i, part].astype(F32)

    arrive(p_recv.at[0], pc.at[0])
    s_buf[0, lo] = both(0, lo).astype(BF16)
    push(s_buf.at[0, lo], via.at[0], via_in.at[0], at_x(1))
    s_buf[0, hi] = both(0, hi).astype(BF16)
    push(s_buf.at[0, hi], via.at[1], via_in.at[1], at_x(-1))
    arrive(p_recv.at[1], pc.at[1])
    s_buf[1, hi] = both(1, hi).astype(BF16)
    push(s_buf.at[1, hi], r_buf.at[0, hi], r_in.at[0, 1], at_x(1))
    arrive(p_recv.at[2], pc.at[2])
    s_buf[2, lo] = both(2, lo).astype(BF16)
    push(s_buf.at[2, lo], r_buf.at[1, lo], r_in.at[1, 0], at_x(-1))
    arrive(via.at[0], via_in.at[0])
    s_buf[1, lo] = (both(1, lo) + via[0].astype(F32)).astype(BF16)
    push(s_buf.at[1, lo], r_buf.at[0, lo], r_in.at[0, 0], at_x(1))
    arrive(via.at[1], via_in.at[1])
    s_buf[2, hi] = (both(2, hi) + via[1].astype(F32)).astype(BF16)
    push(s_buf.at[2, hi], r_buf.at[1, hi], r_in.at[1, 1], at_x(-1))
    arrive(p_recv.at[3], pc.at[3])
    for k in (0, 1):
        arrive(r_buf.at[0, lo if k == 0 else hi], r_in.at[0, k])
        arrive(r_buf.at[1, lo if k == 0 else hi], r_in.at[1, k])

    def summed(begin, size):
        part = pl.ds(begin, size)
        return both(3, part) + r_buf[0, part].astype(F32) + r_buf[1, part].astype(F32)

    count = len(base)
    begin = count
    for k, (size, d) in enumerate(((count, 1), (count, -1), (last, 2), (last, -2))):
        part = pl.ds(begin, size)
        s_buf[3, part] = summed(begin, size).astype(BF16)
        push(s_buf.at[3, part], near.at[pl.ds(begin - count, size)], near_in.at[k], at_z(d))
        begin += size
    begin = 0
    for k, size in enumerate((count, count, last, last)):
        arrive(near.at[pl.ds(begin, size)], near_in.at[k])
        begin += size

    def relayed(j):
        total = own[3, j] + p_recv[3, j].astype(F32) + r_buf[0, j].astype(F32) + r_buf[1, j].astype(F32)
        total = total + near[j].astype(F32) + near[count + j].astype(F32)
        for s in range(last):
            if base[j] == STRIDE * s:
                total = total + near[2 * count + s].astype(F32)
            if base[j] == -STRIDE * s:
                total = total + near[2 * count + last + s].astype(F32)
        return total

    for j in range(count - 1, 0, -1):
        far_send[j] = relayed(j).astype(BF16)
        push(far_send.at[j], far.at[j], far_in.at[j], at_z(base[j]))
    total = relayed(0)
    for j in range(1, count):
        arrive(far.at[j], far_in.at[j])
        total = total + far[j].astype(F32)
    fin[...] = total.astype(BF16)
    push(fin, fin_recv, fin_in, partner)
    out[c] = total.astype(BF16)
    arrive(fin_recv, fin_in)
    out[1 - c] = fin_recv[...]
    for cp in sent:
        cp.wait_send()


def shards(tokens, expert_ids, gate_codes, w_gate, w_up, w_down):
    tok_rows, features = tokens.shape
    owners, tensors, subs = lax.axis_size("expert"), lax.axis_size("tensor"), lax.axis_size("sub")
    blocks = tensors * subs
    width = features // blocks
    runs = w_gate.shape[1]
    chip_rows = tok_rows * subs
    waves, rings, base, order = plan(owners)
    last, count = len(waves) - 1, len(base)

    lane = jnp.arange(LANES, dtype=jnp.int32)
    share = jnp.where(expert_ids[:, :, None] == lane, gate_codes.astype(F32)[:, :, None] / 64.0, 0.0)
    share = jnp.sum(share, axis=1).astype(BF16)
    chunk = tokens.reshape(tok_rows, blocks, width).transpose(1, 0, 2)
    chunk = jnp.concatenate([chunk, jnp.broadcast_to(share, (blocks, tok_rows, LANES))], axis=2)
    mine = (jnp.arange(chip_rows) // tok_rows == lax.axis_index("sub"))[None, :, None]
    placed = jnp.where(mine, jnp.concatenate([chunk] * subs, axis=1), 0)

    def vmem(*shape, dtype=BF16):
        return pltpu.VMEM(shape, dtype)

    tile = (chip_rows, width)
    dma = pltpu.SemaphoreType.DMA
    whole = pl.BlockSpec(memory_space=pltpu.VMEM)
    away = pl.BlockSpec(memory_space=pl.ANY)
    mixed = pl.pallas_call(
        functools.partial(kernel, owners, tensors),
        out_shape=jax.ShapeDtypeStruct((subs,) + tile, BF16),
        in_specs=[whole, away, away, away],
        out_specs=whole,
        scratch_shapes=[
            vmem(owners, chip_rows, width + LANES),
            vmem(chip_rows, width + LANES),
            vmem(3, owners, *tile),
            vmem(4, owners, *tile),
            vmem(blocks, 2 * runs, width),
            vmem(blocks, runs, width),
            vmem(owners * chip_rows, 2 * runs, dtype=F32),
            vmem(4, owners, *tile, dtype=F32),
            vmem(4, owners, *tile),
            vmem(4, owners, *tile),
            vmem(4, owners, *tile),
            vmem(2, owners // 2, *tile),
            vmem(2, owners, *tile),
            vmem(owners - count, *tile),
            vmem(count, *tile),
            vmem(count, *tile),
            vmem(*tile),
            vmem(*tile),
            dma((3 * blocks,)),
            dma((112,)),
            dma,
            dma((last + 1,)),
            dma((last + 1,)),
            dma((last + 1,)),
            dma((2, last + 1)),
            dma((2, last + 1)),
            dma((4, last + 1)),
            dma((4,)),
            dma((2,)),
            dma((2, 2)),
            dma((4,)),
            dma((count,)),
            dma,
        ],
        compiler_params=pltpu.CompilerParams(
            collective_id=0, has_side_effects=True, vmem_limit_bytes=56 * 1024 * 1024
        ),
        name="routed",
    )(placed, w_gate, w_up, w_down)
    start = lax.axis_index("sub") * tok_rows
    kept = lax.dynamic_slice(mixed, (0, start, 0), (subs, tok_rows, width))
    return kept.transpose(1, 0, 2).reshape(tok_rows, subs * width)


def solution(mesh):
    return jax.shard_map(
        shards,
        mesh=mesh,
        in_specs=(
            P(("group", "expert", "sub"), None),
            P(("group", "expert", "sub"), None),
            P(("group", "expert", "sub"), None),
            P("expert", ("tensor", "sub"), None),
            P("expert", ("tensor", "sub"), None),
            P("expert", ("tensor", "sub"), None),
        ),
        out_specs=P(("group", "expert", "sub"), "tensor"),
        check_vma=False,
    )
```

time: 408 us -> 132 us (0.32)
  blocking collectives: 259 us -> 0 us
  Pallas kernels: 0 us -> 126 us
  waiting for transfers between devices: 74 us -> 0 us
  starting transfers between devices: 22.1 us -> 0 us
  local copies, waits for them, and re-layouts: 23.1 us -> 1.37 us
  between operations: 13.5 us -> 0.01 us
  matrix products: 12.2 us -> 0 us
    all_to_all x2 -> x0, blocking collectives: 259 us -> none  [the longest x1 222 us: shards(): lax.all_to_all(outgoing.reshape(owners, capacity, features), 'expert', sp...]
    pallas_call x0 -> x1, Pallas kernels: none -> 126 us  [shards(): pl.pallas_call(functools.partial(kernel, owners, tensors), out_shape=jax....]
    all_to_all x1 -> x0, waiting for transfers between devices: 57.5 us -> none  [shards(): lax.all_to_all(run_total.astype(jnp.bfloat16), 'expert', split_axis=0, co...]
    all_to_all x1 -> x0, starting transfers between devices: 22.1 us -> none  [shards(): lax.all_to_all(run_total.astype(jnp.bfloat16), 'expert', split_axis=0, co...]
    all_gather x1 -> x0, waiting for transfers between devices: 16.4 us -> none  [shards(): lax.all_gather(arrived, 'sub', axis=1, tiled=True).reshape(-1, features)]
    dot_general x4 -> x0, matrix products: 12.2 us -> none  [the longest x1 6.96 us: shards(): jnp.dot(hidden, w_down[0], preferred_element_type=jnp.float32)]
    reshape x3 -> x0, local copies, waits for them, and re-layouts: 7.13 us -> none  [the longest x1 4.62 us: shards(): lax.all_gather(arrived, 'sub', axis=1, tiled=True).reshape(-1, features)]
    another operation x1 -> x0, local copies, waits for them, and re-layouts: 6.22 us -> none  [shards(): partial_value.reshape(owners, sub_count, capacity, tensor_count, block)]
  transfers between devices with their start and end apart: 2 -> 0, of which waited for: 2 -> 0; matrix products, arithmetic and copies ran while one was open for 0% -> 0% of each run, Pallas kernels for 0% -> 0%
where the time goes in v1:
time: 132 us; the launch traced here: 130 us
  Pallas kernels  126 us (95%)
  other arithmetic  3.07 us (2%)
  local copies, waits for them, and re-layouts  1.37 us (1%)
    pallas_call x1, Pallas kernels, shards(): pl.pallas_call(functools.partial(kernel, owners, tensors), out_shape=jax....  126 us

profile of v1, /device:TPU:33, one launch (start us, length us, event | category | flops | bytes accessed | tf_op | source)
XLA Modules:
  0.0 130.2 jit_solution(11730139307796135361)
XLA Ops:
  0.0 0.7 convert_multiply_fusion
  0.7 0.8 select_reduce_fusion
  1.5 1.6 %maximum_select_fusion.placed = bf16[8,8,1024]{2,1,0:T(8,128)(2,1)} fusion(bf16[8,4,128]{2,1,0:T(4,128)(2,1)S(1)} %broadcast_in_dim.34, bf16[8,4,896]{2,1,0:T(4,128)(2,1)} %bitcast.6, pred[8]{0:T(512)(128)(4,1)S(1)} %fusion), kind=kLoop, calls=%fused_computation | loop fusion | flops 589824 | bytes 196616 | tf_op jit(solution)/shard_map/jit(_where)/select_n | solution.py:288
  3.1 125.8 %routed.1 = bf16[2,8,896]{2,1,0:T(8,128)(2,1)} custom-call(bf16[8,8,1024]{2,1,0:T(8,128)(2,1)} %maximum_select_fusion.placed, bf16[1,128,7168]{2,1,0:T(8,128)(2,1)} %w_gate.1, bf16[1,128,7168]{2,1,0:T(8,128)(2,1)} %w_up.1, bf16[1,128,7168]{2,1,0:T(8,128)(2,1)} %w_down.1), custom_call_target="tpu_custom_call" | custom-call | tf_op jit(solution)/shard_map/routed/pallas_call | solution.py:297
  128.9 1.4 %constant_dynamic-slice_fusion = bf16[2,4,896]{2,1,0:T(4,128)(2,1)} fusion(bf16[2,8,896]{2,1,0:T(8,128)(2,1)} %routed.1, s32[]{:T(128)S(6)} %select_n.23), kind=kLoop, calls=%fused_computation.9 | loop fusion | bytes 28676 | tf_op jit(solution)/shard_map/dynamic_slice | solution.py:343
  (2 shorter events, 0.0 us)
